TPU v7x, 256 devices: a whole 4x4x8 slice. The times are simulated.
256 devices in a mesh: ctx: 8 (over z), exp: 32 (over x, y, core).
Axes of the slice: x: 4, y: 4, z: 8, core: 2. Of those that a mesh axis runs over, the one named last changes fastest.
Arguments:
- q_latent: bfloat16 [128, 128, 512], P('exp'), may hold values from -7 to 7
- q_rope: bfloat16 [128, 64, 128], P('exp'), may hold values from -84 to 84
- cache_latent: bfloat16 [128, 4096, 512], P('exp', 'ctx'), may hold values from -6 to 6
- cache_rope: bfloat16 [128, 64, 4096], P('exp', None, 'ctx'), may hold values from -6 to 6
- lengths: int32 [128], P('exp'), may hold values from 1024 to 4096
- w_attn_out: bfloat16 [128, 512, 7168], P('ctx', None, 'exp'), may hold values from -0.1875 to 0.1875
- hidden_in: bfloat16 [128, 7168], P(None, 'exp'), may hold values from -6 to 6
- norm_gain: bfloat16 [7168], replicated, may hold values from 0.5 to 8
- w_gate: bfloat16 [32, 7168, 1024], P('exp', None, 'ctx'), may hold values from -0.0625 to 0.0625
- w_up: bfloat16 [32, 7168, 1024], P('exp', None, 'ctx'), may hold values from -0.0625 to 0.0625
- w_down: bfloat16 [32, 1024, 7168], P('exp', 'ctx'), may hold values from -0.1875 to 0.1875
- expert_ids: int32 [128, 8], replicated, may hold values from 0 to 31, all different within a row; in each aligned block of 128 rows (0 to 127, 128 to 255, ...) at most 64 rows name the same one
- gate_weights: float32 [128, 8], replicated, may hold values from 0.1 to 1
Outputs:
- layer_out: bfloat16 [128, 7168], P('exp', 'ctx')
Inputs may be any that keep to these rules, and one draw needn't show every extreme that they name: `expert_ids`: each row names 8 different experts; over all 128 rows no expert is named more than 64 times, a bound that some block reaches.
All inputs are finite; a program needn't handle non-finite values.
Results may differ from a plain program's by a relative error of at most 0.008.
Values may be sent and summed in bfloat16 or wider, within the bound.
A program may use at most 64 MiB of HBM per device.

v0:
```python
import math
import jax
import jax.numpy as jnp
from jax import lax
from jax.sharding import PartitionSpec as P

SOFTMAX_SCALE = 192.0 ** (-0.5)
MASKED = -1e30
EPSILON = 1e-06


def cut_along(array, dim, devices):
    before, after = (array.shape[:dim], array.shape[dim + 1 :])
    return jnp.moveaxis(array.reshape(*before, devices, -1, *after), dim, 0)


def summed_on_arrival(array, axis, dim):
    devices = lax.axis_size(axis)
    blocks = lax.all_to_all(cut_along(array, dim, devices), axis, 0, 0, tiled=True)
    return jnp.sum(blocks, axis=0)


def sent_together(arrays, axis, dim, along):
    widths = [math.prod(a.shape[along:]) for a in arrays]
    both = jnp.concatenate(
        [a.reshape(*a.shape[:along], w) for a, w in zip(arrays, widths)], axis=along
    )
    filled = summed_on_arrival(both, axis, dim)
    blocks = jnp.split(filled, [sum(widths[:k]) for k in range(1, len(widths))], axis=along)
    return tuple(
        (b.reshape(*filled.shape[:along], *a.shape[along:]) for a, b in zip(arrays, blocks))
    )


def copy_for_each(array, axis):
    copies = jnp.broadcast_to(array, (lax.axis_size(axis), *array.shape))
    return lax.all_to_all(copies, axis, split_axis=0, concat_axis=0, tiled=True)


def taken_together(array, axis):
    everything = copy_for_each(array, axis)
    return jnp.sum(everything, axis=0)


def slot_tables(expert_ids, gate_weights, experts, capacity):
    row_count, top_count = expert_ids.shape
    flat_ids = expert_ids.reshape(-1)
    one_hot = (flat_ids[:, None] == jnp.arange(experts, dtype=jnp.int32)[None, :]).astype(jnp.int32)
    before = jnp.cumsum(one_hot, axis=0) - one_hot
    slot_index = jnp.sum(before * one_hot, axis=1)
    target = flat_ids * capacity + slot_index
    owner_row = jnp.arange(row_count * top_count, dtype=jnp.int32) // top_count
    slot_row = jnp.full((experts * capacity,), row_count, jnp.int32).at[target].set(owner_row)
    slot_gate = (
        jnp.zeros((experts * capacity,), jnp.float32).at[target].set(gate_weights.reshape(-1))
    )
    return (slot_row, slot_gate)


def per_device(
    q_latent,
    q_rope,
    cache_latent,
    cache_rope,
    lengths,
    w_attn_out,
    hidden_in,
    norm_gain,
    w_gate,
    w_up,
    w_down,
    expert_ids,
    gate_weights,
):
    ctx_index = lax.axis_index("ctx")
    exp_index = lax.axis_index("exp")
    ctx_count = lax.axis_size("ctx")
    exp_count = lax.axis_size("exp")
    block_len = cache_latent.shape[1]
    positions = ctx_index * block_len + jnp.arange(block_len, dtype=jnp.int32)
    visible = positions[None, :] < lengths[:, None]
    scores = jnp.einsum("rhl,rpl->rhp", q_latent, cache_latent, preferred_element_type=jnp.float32)
    scores = (
        scores + jnp.einsum("rdh,rdp->rhp", q_rope, cache_rope, preferred_element_type=jnp.float32)
    ) * SOFTMAX_SCALE
    scores = jnp.where(visible[:, None, :], scores, MASKED)
    block_max = jnp.max(scores, axis=2)
    weights = jnp.where(visible[:, None, :], jnp.exp(scores - block_max[..., None]), 0.0)
    block_total = jnp.sum(weights, axis=2)
    block_value = jnp.einsum(
        "rhp,rpl->rhl",
        weights.astype(jnp.bfloat16),
        cache_latent,
        preferred_element_type=jnp.float32,
    )
    head_count = w_attn_out.shape[0]
    joint_max = lax.pmax(block_max, "ctx")
    rescale = jnp.exp(block_max - joint_max)
    share_total, share_value = sent_together(
        (block_total * rescale, block_value * rescale[..., None]), "ctx", 1, 2
    )
    attended = (share_value / share_total[..., None]).astype(jnp.bfloat16)
    latent_width = w_attn_out.shape[1]
    flat_weight = w_attn_out.reshape(head_count * latent_width, w_attn_out.shape[2])
    row_piece = lax.all_gather(attended, "exp", axis=0, tiled=True)
    partial_out = jnp.dot(
        row_piece.reshape(row_piece.shape[0], head_count * latent_width),
        flat_weight,
        preferred_element_type=jnp.float32,
    )
    hidden_state = hidden_in.astype(jnp.float32) + taken_together(partial_out, "ctx")
    row_count = hidden_in.shape[0]
    share_width = hidden_in.shape[1]
    model_width = share_width * exp_count
    column_width = model_width // ctx_count
    top_count = expert_ids.shape[1]
    local_experts = w_gate.shape[0]
    experts = exp_count * local_experts
    capacity = min(row_count, 2 * row_count * top_count // experts)
    slot_row, slot_gate = slot_tables(expert_ids, gate_weights, experts, capacity)
    rounded = hidden_state.astype(jnp.bfloat16)
    padded = jnp.concatenate([rounded, jnp.zeros((1, share_width), jnp.bfloat16)], axis=0)
    outbound = padded[slot_row].reshape(experts, capacity, share_width)
    values = lax.all_to_all(outbound, "exp", split_axis=0, concat_axis=2, tiled=True).astype(
        jnp.float32
    )
    mean_square = jnp.mean(values * values, axis=2, keepdims=True)
    normed = (values * lax.rsqrt(mean_square + EPSILON) * norm_gain.astype(jnp.float32)).astype(
        jnp.bfloat16
    )
    gate_part = jnp.einsum("end,edf->enf", normed, w_gate, preferred_element_type=jnp.float32)
    up_part = jnp.einsum("end,edf->enf", normed, w_up, preferred_element_type=jnp.float32)
    active = (jax.nn.silu(gate_part) * up_part).astype(jnp.bfloat16)
    expert_part = jnp.einsum("enf,efd->end", active, w_down, preferred_element_type=jnp.float32)
    local_rows = lax.dynamic_slice_in_dim(
        slot_row, exp_index * local_experts * capacity, local_experts * capacity
    )
    local_gates = lax.dynamic_slice_in_dim(
        slot_gate, exp_index * local_experts * capacity, local_experts * capacity
    )
    weighted = expert_part.reshape(local_experts * capacity, model_width) * local_gates[:, None]
    owner_block = exp_index * share_width // column_width
    offset = exp_index * share_width % column_width
    column_part = summed_on_arrival(weighted, "ctx", 1)
    summed = jax.ops.segment_sum(column_part, local_rows, num_segments=row_count)
    current = lax.dynamic_slice(summed, (0, offset), (row_count, share_width))
    residual = jnp.where(ctx_index == owner_block, hidden_state, 0.0)
    summed = lax.dynamic_update_slice(summed, current + residual, (0, offset))
    layer_out = summed_on_arrival(summed, "exp", 0)
    return layer_out.astype(jnp.bfloat16)


def solution(mesh):
    in_specs = (
        P("exp", None, None),
        P("exp", None, None),
        P("exp", "ctx", None),
        P("exp", None, "ctx"),
        P("exp"),
        P("ctx", None, "exp"),
        P(None, "exp"),
        P(),
        P("exp", None, "ctx"),
        P("exp", None, "ctx"),
        P("exp", "ctx", None),
        P(),
        P(),
    )
    out_specs = P("exp", "ctx")
    return jax.shard_map(
        per_device, mesh=mesh, in_specs=in_specs, out_specs=out_specs, check_vma=False
    )
```

profile of v0, /device:TPU:1, one launch (start us, length us, event | category | flops | bytes accessed | tf_op | source)
XLA Modules:
  0.0 277.0 jit_solution(6442682698349328505)
XLA Ops:
  8.1 1.9 fusion.58
  10.5 17.3 %pmax.7 = f32[4,128]{1,0:T(4,128)S(1)} all-reduce(f32[4,128]{1,0:T(4,128)S(1)} %get-tuple-element.7), channel_id=1, replica_groups=mesh['ctx'=8,'exp'=32] {'ctx'}, use_global_device_ids=true, to_apply=%region_6.7 | all-reduce | flops 512 | bytes 4096 | tf_op jit(solution)/shard_map/pmax | solution.py:97
  30.0 1.6 maximum_bitcast_fusion
  31.7 31.7 %all_to_all.29 = f32[8,4,16,513]{3,2,1,0:T(8,128)S(1)} all-to-all(f32[8,4,16,513]{3,2,1,0:T(8,128)S(1)} %maximum_bitcast_fusion), channel_id=1, replica_groups=mesh['ctx'=8,'exp'=32] {'ctx'}, dimensions={0} | all-to-all | bytes 2101248 | tf_op jit(solution)/shard_map/all_to_all | solution.py:19
  64.9 1.6 fusion.37
  66.6 51.4 %all-gather.2.cloned.1.call-done = bf16[128,16,512]{2,1,0:T(8,128)(2,1)} async-done(((bf16[4,16,512]{2,1,0:T(8,128)(2,1)}), bf16[128,16,512]{2,1,0:T(8,128)(2,1)}) %all-gather.2.cloned.1.call-update) | async-done | bytes 2097168 | tf_op jit(solution)/shard_map/all_gather | solution.py:105
  118.0 5.2 %fusion.11 = f32[128,224]{0,1:T(8,128)S(1)} fusion(bf16[16,512,224]{1,2,0:T(8,128)(2,1)} %param.18, bf16[128,16,512]{2,1,0:T(8,128)(2,1)} %all-gather.2.cloned.1.call-done), kind=kOutput, calls=%fused_computation.21 | convolution fusion | flops 469762048 | bytes 5881856 | tf_op jit(solution)/shard_map/dot_general | solution.py:106
  124.2 6.7 %all-to-all-start.1 = ((f32[8,128,224]{1,2,0:T(8,128)}), f32[8,128,224]{1,2,0:T(8,128)S(1)}, u32[]{:S(2)}, u32[]{:S(2)}) async-start(f32[8,128,224]{1,2,0:T(8,128)} %broadcast_in_dim.59), calls=%async_computation.1 | async-start | bytes 1835008 | tf_op jit(solution)/shard_map/all_to_all | solution.py:37
  131.6 9.0 %reduce-window.6 = s32[32,8,128]{2,1,0:T(8,128)S(1)} reduce-window(s32[32,8,128]{2,1,0:T(8,128)S(1)} %fusion.38, s32[]{:T(128)} %constant.34.clone.1), window={size=1x1x128 pad=0_0x0_0x127_0}, to_apply=%region_0.1 | reduce-window | flops 4161536 | bytes 262148 | tf_op jit(solution)/shard_map/reduce-window
  141.1 4.3 %scatter_custom_fusion = s32[2048]{0:T(1024)S(1)} fusion(s32[1024]{0:T(1024)S(1)} %bitcast.76, s32[1024]{0:T(1024)S(1)} %add_select_fusion, s32[]{:T(128)} %constant.31.clone.1), kind=kCustom, calls=%fused_computation.66 | custom fusion | bytes 8196 | tf_op jit(solution)/shard_map/scatter | solution.py:53
  145.5 11.9 %all-to-all-done.1 = f32[8,128,224]{1,2,0:T(8,128)S(1)} async-done(((f32[8,128,224]{1,2,0:T(8,128)}), f32[8,128,224]{1,2,0:T(8,128)S(1)}, u32[]{:S(2)}, u32[]{:S(2)}) %all-to-all-start.1) | async-done | bytes 917536 | tf_op jit(solution)/shard_map/all_to_all | solution.py:37
  157.5 9.0 %gather_fusion = bf16[2048,224]{1,0:T(8,128)(2,1)} fusion(bf16[129,224]{1,0:T(8,128)(2,1)S(1)} %concatenate.14, s32[2048]{0:T(1024)S(1)} %fusion.46), kind=kCustom, calls=%fused_computation | custom fusion | bytes 1843200 | tf_op jit(solution)/shard_map/gather | solution.py:123
  166.5 5.6 %all-to-all-start.2 = ((bf16[32,64,224]{2,1,0:T(8,128)(2,1)}), bf16[32,64,224]{2,1,0:T(8,128)(2,1)S(1)}, u32[]{:S(2)}, u32[]{:S(2)}) async-start(bf16[32,64,224]{2,1,0:T(8,128)(2,1)} %bitcast.71), calls=%async_computation.2 | async-start | bytes 2097152 | tf_op jit(solution)/shard_map/all_to_all | solution.py:124
  172.4 4.5 %scatter_custom_fusion.1 = f32[2048]{0:T(1024)S(1)} fusion(s32[1024]{0:T(1024)S(1)} %bitcast.77, f32[1024]{0:T(1024)S(1)} %reshape.230, f32[]{:T(128)} %constant.28.clone.1), kind=kCustom, calls=%fused_computation.63 | custom fusion | bytes 8196 | tf_op jit(solution)/shard_map/scatter | solution.py:55
  176.9 3.9 %copy.72 = bf16[7168,128]{1,0:T(8,128)(2,1)} copy(bf16[7168,128]{0,1:T(8,128)(2,1)} %bitcast.72) | data formatting | bytes 3670016 | tf_op jit(solution)/shard_map/enf,efd->end/dot_general | solution.py:134
  180.9 8.1 %all-to-all-done.2 = bf16[32,64,224]{2,1,0:T(8,128)(2,1)S(1)} async-done(((bf16[32,64,224]{2,1,0:T(8,128)(2,1)}), bf16[32,64,224]{2,1,0:T(8,128)(2,1)S(1)}, u32[]{:S(2)}, u32[]{:S(2)}) %all-to-all-start.2) | async-done | bytes 917536 | tf_op jit(solution)/shard_map/all_to_all | solution.py:124
  189.7 1.6 copy.69
  191.3 2.6 convert_element_type.70
  193.9 2.0 fusion.7
  195.9 4.5 %multiply_bitcast_fusion = f32[8,64,896]{2,1,0:T(8,128)} fusion(bf16[8,896,128]{2,1,0:T(8,128)(2,1)} %bitcast.69, f32[64]{0:T(128)S(1)} %dynamic_slice.10, bf16[64,7168]{1,0:T(8,128)(2,1)S(1)} %convert_element_type.70, bf16[1,7168,128]{2,1,0:T(8,128)(2,1)} %param.22, f32[64,128]{1,0:T(8,128)S(1)} %fusion.7), kind=kOutput, calls=%fused_computation.15 | convolution fusion | flops 235388928 | bytes 6455552 | tf_op jit(solution)/shard_map/enf,efd->end/dot_general | solution.py:134
  200.4 4.3 %all-to-all-start.3 = ((f32[8,64,896]{2,1,0:T(8,128)}), f32[8,64,896]{2,1,0:T(8,128)}, u32[]{:S(2)}, u32[]{:S(2)}) async-start(f32[8,64,896]{2,1,0:T(8,128)} %multiply_bitcast_fusion), calls=%async_computation.3 | async-start | bytes 3670016 | tf_op jit(solution)/shard_map/all_to_all | solution.py:19
  204.8 43.0 %all-to-all-done.3 = f32[8,64,896]{2,1,0:T(8,128)} async-done(((f32[8,64,896]{2,1,0:T(8,128)}), f32[8,64,896]{2,1,0:T(8,128)}, u32[]{:S(2)}, u32[]{:S(2)}) %all-to-all-start.3) | async-done | bytes 1835040 | tf_op jit(solution)/shard_map/all_to_all | solution.py:19
  247.8 1.6 reduce_sum.71
  252.2 17.2 %all_to_all.30 = f32[32,4,896]{2,1,0:T(4,128)S(1)} all-to-all(f32[32,4,896]{2,1,0:T(4,128)S(1)} %reshape.207), channel_id=1, replica_groups=mesh['ctx'=8,'exp'=32] {'exp'}, dimensions={0} | all-to-all | bytes 917504 | tf_op jit(solution)/shard_map/all_to_all | solution.py:19
  (62 shorter events, 12.7 us)
Async XLA Ops:
  6.5 1.6 copy-start
  6.5 111.4 %all-gather.2.cloned.1.call-start = ((), (), s32[]{:S(2)}) async-start(), calls=%async_computation.5 | async-start | bytes 2162688 | tf_op jit(solution)/shard_map/all_gather | solution.py:105
  8.1 1.9 copy-start.1
  8.1 1.9 copy-start.2
  123.2 7.7 %copy-start.4 = (s32[128,8]{0,1:T(8,128)S(1)}, s32[128,8]{0,1:T(8,128)}, u32[]{:S(2)}) copy-start(s32[128,8]{0,1:T(8,128)} %param.24) | copy-start | bytes 12292
  123.2 8.2 %copy-start.3 = (bf16[128,224]{0,1:T(8,128)(2,1)S(1)}, bf16[128,224]{0,1:T(8,128)(2,1)}, u32[]{:S(2)}) copy-start(bf16[128,224]{0,1:T(8,128)(2,1)} %param.19) | copy-start | bytes 172036
  124.2 33.1 %all-to-all-start.1 = ((f32[8,128,224]{1,2,0:T(8,128)}), f32[8,128,224]{1,2,0:T(8,128)S(1)}, u32[]{:S(2)}, u32[]{:S(2)}) async-start(f32[8,128,224]{1,2,0:T(8,128)} %broadcast_in_dim.59), calls=%async_computation.1 | async-start | bytes 1835008 | tf_op jit(solution)/shard_map/all_to_all | solution.py:37
  166.5 5.6 %copy-start.5 = (bf16[7168]{0:T(1024)(128)(2,1)S(1)}, bf16[7168]{0:T(1024)(128)(2,1)}, u32[]{:S(2)}) copy-start(bf16[7168]{0:T(1024)(128)(2,1)} %param.20) | copy-start | bytes 43012
  166.5 5.7 %copy-start.6 = (f32[128,8]{0,1:T(8,128)S(1)}, f32[128,8]{0,1:T(8,128)}, u32[]{:S(2)}) copy-start(f32[128,8]{0,1:T(8,128)} %param.25) | copy-start | bytes 12292
  166.5 22.5 %all-to-all-start.2 = ((bf16[32,64,224]{2,1,0:T(8,128)(2,1)}), bf16[32,64,224]{2,1,0:T(8,128)(2,1)S(1)}, u32[]{:S(2)}, u32[]{:S(2)}) async-start(bf16[32,64,224]{2,1,0:T(8,128)(2,1)} %bitcast.71), calls=%async_computation.2 | async-start | bytes 2097152 | tf_op jit(solution)/shard_map/all_to_all | solution.py:124
  200.4 47.5 %all-to-all-start.3 = ((f32[8,64,896]{2,1,0:T(8,128)}), f32[8,64,896]{2,1,0:T(8,128)}, u32[]{:S(2)}, u32[]{:S(2)}) async-start(f32[8,64,896]{2,1,0:T(8,128)} %multiply_bitcast_fusion), calls=%async_computation.3 | async-start | bytes 3670016 | tf_op jit(solution)/shard_map/all_to_all | solution.py:19
Sparse Core Ops, SparseCore 0:
  66.7 51.2 all-gather.1
where the time goes:
time: 278 us; the launch traced here: 277 us
  waiting for transfers between devices  114 us (41%)
  blocking collectives  66.1 us (24%)
  local copies, waits for them, and re-layouts  31.7 us (11%)
  other arithmetic  18.8 us (7%)
  starting transfers between devices  16.6 us (6%)
  matrix products  15.6 us (6%)
  between operations  13.7 us (5%)
    all_gather x1, waiting for transfers between devices, per_device(): row_piece = lax.all_gather(attended, 'exp', axis=0, tiled=True)  51.4 us
    all_to_all x2, blocking collectives, summed_on_arrival(): lax.all_to_all(cut_along(array, dim, devices), axis, 0, 0, tiled=True)  48.9 us
    all_to_all x1, waiting for transfers between devices, summed_on_arrival(): lax.all_to_all(cut_along(array, dim, devices), axis, 0, 0, tiled=True)  43 us
    pmax x1, blocking collectives, per_device(): joint_max = lax.pmax(block_max, 'ctx')  17.3 us
    all_to_all x1, waiting for transfers between devices, copy_for_each(): return lax.all_to_all(copies, axis, split_axis=0, concat_axis=0, tiled=True)  11.9 us
    another operation x3, other arithmetic  9.15 us
    gather x1, local copies, waits for them, and re-layouts, per_device(): outbound = padded[slot_row].reshape(experts, capacity, share_width)  9 us
    all_to_all x1, waiting for transfers between devices, per_device(): lax.all_to_all(outbound, 'exp', split_axis=0, concat_axis=2, tiled=True)  8.11 us
  transfers between devices with their start and end apart: 4, of which 4 were waited for; matrix products, arithmetic and copies ran while one was open for 8% of the time, Pallas kernels for 0%

commit v1 on v0

--- a/solution.py
+++ b/solution.py
@@ -102,7 +102,11 @@
     attended = (share_value / share_total[..., None]).astype(jnp.bfloat16)
     latent_width = w_attn_out.shape[1]
     flat_weight = w_attn_out.reshape(head_count * latent_width, w_attn_out.shape[2])
-    row_piece = lax.all_gather(attended, "exp", axis=0, tiled=True)
+    size = lax.axis_size("exp")
+    repeats = [size if d == 0 else 1 for d in range(attended.ndim)]
+    row_piece = lax.all_to_all(
+        jnp.tile(attended, repeats), "exp", split_axis=0, concat_axis=0, tiled=True
+    )
     partial_out = jnp.dot(
         row_piece.reshape(row_piece.shape[0], head_count * latent_width),
         flat_weight,

time: 278 us -> 247 us (0.89)
  waiting for transfers between devices: 114 us -> 63.1 us
  blocking collectives: 66.1 us -> 108 us
  between operations: 13.7 us -> 0.34 us
  starting transfers between devices: 16.6 us -> 12 us
  matrix products: 15.6 us -> 12.8 us
    all_gather x1 -> x0, waiting for transfers between devices: 51.4 us -> none  [per_device(): row_piece = lax.all_gather(attended, 'exp', axis=0, tiled=True)]
    all_to_all x0 -> x1, blocking collectives: none -> 41.9 us  [per_device(): lax.all_to_all(jnp.tile(attended, repeats), 'exp', split_axis=0, concat_a...]
    all_to_all x1, starting transfers between devices: 6.73 us -> 3.55 us  [copy_for_each(): return lax.all_to_all(copies, axis, split_axis=0, concat_axis=0, tiled=True)]
  transfers between devices with their start and end apart: 4 -> 3, of which waited for: 4 -> 3; matrix products, arithmetic and copies ran while one was open for 8% -> 9% of each run, Pallas kernels for 0% -> 0%
where the time goes in v1:
time: 247 us; the launch traced here: 246 us
  blocking collectives  108 us (44%)
  waiting for transfers between devices  63.1 us (26%)
  local copies, waits for them, and re-layouts  31.9 us (13%)
  other arithmetic  18.2 us (7%)
  matrix products  12.8 us (5%)
  starting transfers between devices  12 us (5%)
    all_to_all x2, blocking collectives, summed_on_arrival(): lax.all_to_all(cut_along(array, dim, devices), axis, 0, 0, tiled=True)  48.9 us
    all_to_all x1, waiting for transfers between devices, summed_on_arrival(): lax.all_to_all(cut_along(array, dim, devices), axis, 0, 0, tiled=True)  43.1 us
    all_to_all x1, blocking collectives, per_device(): lax.all_to_all(jnp.tile(attended, repeats), 'exp', split_axis=0, concat_a...  41.9 us
    pmax x1, blocking collectives, per_device(): joint_max = lax.pmax(block_max, 'ctx')  17.3 us
    all_to_all x1, waiting for transfers between devices, copy_for_each(): return lax.all_to_all(copies, axis, split_axis=0, concat_axis=0, tiled=True)  11.8 us
    another operation x3, other arithmetic  9.14 us
    gather x1, local copies, waits for them, and re-layouts, per_device(): outbound = padded[slot_row].reshape(experts, capacity, share_width)  9 us
    all_to_all x1, waiting for transfers between devices, per_device(): lax.all_to_all(outbound, 'exp', split_axis=0, concat_axis=2, tiled=True)  8.21 us
  transfers between devices with their start and end apart: 3, of which 3 were waited for; matrix products, arithmetic and copies ran while one was open for 9% of the time, Pallas kernels for 0%

profile of v1, /device:TPU:1, one launch (start us, length us, event | category | flops | bytes accessed | tf_op | source)
XLA Modules:
  0.0 246.5 jit_solution(12845880481138988821)
XLA Ops:
  1.6 1.8 fusion.58
  3.9 17.3 %pmax.7 = f32[4,128]{1,0:T(4,128)S(1)} all-reduce(f32[4,128]{1,0:T(4,128)S(1)} %get-tuple-element.7), channel_id=1, replica_groups=mesh['ctx'=8,'exp'=32] {'ctx'}, use_global_device_ids=true, to_apply=%region_6.7 | all-reduce | flops 512 | bytes 4096 | tf_op jit(solution)/shard_map/pmax | solution.py:97
  21.5 1.6 convolution_multiply_fusion
  23.5 1.6 maximum_bitcast_fusion
  25.1 31.7 %all_to_all.34 = f32[8,4,16,513]{3,2,1,0:T(8,128)S(1)} all-to-all(f32[8,4,16,513]{3,2,1,0:T(8,128)S(1)} %maximum_bitcast_fusion), channel_id=1, replica_groups=mesh['ctx'=8,'exp'=32] {'ctx'}, dimensions={0} | all-to-all | bytes 2101248 | tf_op jit(solution)/shard_map/all_to_all | solution.py:19
  59.6 41.9 %all_to_all.35 = bf16[128,16,512]{2,1,0:T(8,128)(2,1)S(1)} all-to-all(bf16[128,16,512]{2,1,0:T(8,128)(2,1)S(1)} %bitcast.68), channel_id=1, replica_groups=mesh['ctx'=8,'exp'=32] {'exp'}, dimensions={0} | all-to-all | bytes 4194304 | tf_op jit(solution)/shard_map/all_to_all | solution.py:107
  101.5 2.6 %fusion.11 = f32[128,224]{0,1:T(8,128)S(1)} fusion(bf16[16,512,224]{1,2,0:T(8,128)(2,1)S(1)} %copy-done.7, bf16[128,16,512]{2,1,0:T(8,128)(2,1)S(1)} %all_to_all.35), kind=kOutput, calls=%fused_computation.21 | convolution fusion | flops 469762048 | bytes 5881856 | tf_op jit(solution)/shard_map/dot_general | solution.py:110
  105.1 3.6 %all-to-all-start.2 = ((f32[8,128,224]{1,2,0:T(8,128)}), f32[8,128,224]{1,2,0:T(8,128)S(1)}, u32[]{:S(2)}, u32[]{:S(2)}) async-start(f32[8,128,224]{1,2,0:T(8,128)} %broadcast_in_dim.59), calls=%async_computation.2 | async-start | bytes 1835008 | tf_op jit(solution)/shard_map/all_to_all | solution.py:37
  109.1 9.0 %reduce-window.6 = s32[32,8,128]{2,1,0:T(8,128)S(1)} reduce-window(s32[32,8,128]{2,1,0:T(8,128)S(1)} %fusion.38, s32[]{:T(128)} %constant.34.clone.1), window={size=1x1x128 pad=0_0x0_0x127_0}, to_apply=%region_0.1 | reduce-window | flops 4161536 | bytes 262148 | tf_op jit(solution)/shard_map/reduce-window
  118.8 4.3 %scatter_custom_fusion = s32[2048]{0:T(1024)S(1)} fusion(s32[1024]{0:T(1024)S(1)} %bitcast.76, s32[1024]{0:T(1024)S(1)} %add_select_fusion, s32[]{:T(128)} %constant.31.clone.1), kind=kCustom, calls=%fused_computation.66 | custom fusion | bytes 8196 | tf_op jit(solution)/shard_map/scatter | solution.py:53
  123.2 11.8 %all-to-all-done.2 = f32[8,128,224]{1,2,0:T(8,128)S(1)} async-done(((f32[8,128,224]{1,2,0:T(8,128)}), f32[8,128,224]{1,2,0:T(8,128)S(1)}, u32[]{:S(2)}, u32[]{:S(2)}) %all-to-all-start.2) | async-done | bytes 917536 | tf_op jit(solution)/shard_map/all_to_all | solution.py:37
  135.2 9.0 %gather_fusion = bf16[2048,224]{1,0:T(8,128)(2,1)} fusion(bf16[129,224]{1,0:T(8,128)(2,1)S(1)} %concatenate.14, s32[2048]{0:T(1024)S(1)} %fusion.46), kind=kCustom, calls=%fused_computation | custom fusion | bytes 1843200 | tf_op jit(solution)/shard_map/gather | solution.py:127
  144.2 4.2 %all-to-all-start.3 = ((bf16[32,64,224]{2,1,0:T(8,128)(2,1)}), bf16[32,64,224]{2,1,0:T(8,128)(2,1)S(1)}, u32[]{:S(2)}, u32[]{:S(2)}) async-start(bf16[32,64,224]{2,1,0:T(8,128)(2,1)} %bitcast.71), calls=%async_computation.3 | async-start | bytes 2097152 | tf_op jit(solution)/shard_map/all_to_all | solution.py:128
  148.6 4.5 %scatter_custom_fusion.1 = f32[2048]{0:T(1024)S(1)} fusion(s32[1024]{0:T(1024)S(1)} %bitcast.77, f32[1024]{0:T(1024)S(1)} %reshape.234, f32[]{:T(128)} %constant.28.clone.1), kind=kCustom, calls=%fused_computation.63 | custom fusion | bytes 8196 | tf_op jit(solution)/shard_map/scatter | solution.py:55
  153.2 3.9 %copy.70 = bf16[7168,128]{1,0:T(8,128)(2,1)} copy(bf16[7168,128]{0,1:T(8,128)(2,1)} %bitcast.72) | data formatting | bytes 3670016 | tf_op jit(solution)/shard_map/enf,efd->end/dot_general | solution.py:138
  157.1 8.2 %all-to-all-done.3 = bf16[32,64,224]{2,1,0:T(8,128)(2,1)S(1)} async-done(((bf16[32,64,224]{2,1,0:T(8,128)(2,1)}), bf16[32,64,224]{2,1,0:T(8,128)(2,1)S(1)}, u32[]{:S(2)}, u32[]{:S(2)}) %all-to-all-start.3) | async-done | bytes 917536 | tf_op jit(solution)/shard_map/all_to_all | solution.py:128
  166.1 1.6 copy.67
  167.6 2.6 %convert_element_type.70 = bf16[64,7168]{1,0:T(8,128)(2,1)S(1)} reshape(bf16[1,64,32,224]{3,2,1,0:T(8,128)(2,1)} %copy.67) | data formatting | bytes 1835008 | tf_op jit(solution)/shard_map/convert_element_type | solution.py:132
  170.3 2.0 fusion.7
  172.2 4.5 %multiply_bitcast_fusion = f32[8,64,896]{2,1,0:T(8,128)} fusion(bf16[8,896,128]{2,1,0:T(8,128)(2,1)} %bitcast.69, f32[64]{0:T(128)S(1)} %dynamic_slice.10, bf16[64,7168]{1,0:T(8,128)(2,1)S(1)} %convert_element_type.70, bf16[1,7168,128]{2,1,0:T(8,128)(2,1)} %param.22, f32[64,128]{1,0:T(8,128)S(1)} %fusion.7), kind=kOutput, calls=%fused_computation.15 | convolution fusion | flops 235388928 | bytes 6455552 | tf_op jit(solution)/shard_map/enf,efd->end/dot_general | solution.py:138
  176.7 4.3 %all-to-all-start.4 = ((f32[8,64,896]{2,1,0:T(8,128)}), f32[8,64,896]{2,1,0:T(8,128)}, u32[]{:S(2)}, u32[]{:S(2)}) async-start(f32[8,64,896]{2,1,0:T(8,128)} %multiply_bitcast_fusion), calls=%async_computation.4 | async-start | bytes 3670016 | tf_op jit(solution)/shard_map/all_to_all | solution.py:19
  181.1 43.1 %all-to-all-done.4 = f32[8,64,896]{2,1,0:T(8,128)} async-done(((f32[8,64,896]{2,1,0:T(8,128)}), f32[8,64,896]{2,1,0:T(8,128)}, u32[]{:S(2)}, u32[]{:S(2)}) %all-to-all-start.4) | async-done | bytes 1835040 | tf_op jit(solution)/shard_map/all_to_all | solution.py:19
  224.2 1.6 reduce_sum.71
  228.5 17.2 %all_to_all.36 = f32[32,4,896]{2,1,0:T(4,128)S(1)} all-to-all(f32[32,4,896]{2,1,0:T(4,128)S(1)} %reshape.211), channel_id=1, replica_groups=mesh['ctx'=8,'exp'=32] {'exp'}, dimensions={0} | all-to-all | bytes 917504 | tf_op jit(solution)/shard_map/all_to_all | solution.py:19
  (63 shorter events, 12.4 us)
Async XLA Ops:
  0.0 1.6 copy-start
  0.0 3.5 %copy-start.2 = (bf16[4,64,128]{2,1,0:T(8,128)(2,1)S(1)}, bf16[4,64,128]{2,1,0:T(8,128)(2,1)}, u32[]{:S(2)}) copy-start(bf16[4,64,128]{2,1,0:T(8,128)(2,1)} %param.14) | copy-start | bytes 196612
  0.0 3.5 %copy-start.1 = (bf16[4,64,512]{2,1,0:T(8,128)(2,1)S(1)}, bf16[4,64,512]{2,1,0:T(8,128)(2,1)}, u32[]{:S(2)}) copy-start(bf16[4,64,512]{2,1,0:T(8,128)(2,1)} %param.16) | copy-start | bytes 786436
  59.6 41.9 %copy-start.7 = (bf16[16,512,224]{1,2,0:T(8,128)(2,1)S(1)}, bf16[16,512,224]{1,2,0:T(8,128)(2,1)}, u32[]{:S(2)}) copy-start(bf16[16,512,224]{1,2,0:T(8,128)(2,1)} %param.18) | copy-start | bytes 11010052
  104.1 4.6 %copy-start.4 = (s32[128,8]{0,1:T(8,128)S(1)}, s32[128,8]{0,1:T(8,128)}, u32[]{:S(2)}) copy-start(s32[128,8]{0,1:T(8,128)} %param.24) | copy-start | bytes 12292
  104.1 4.9 %copy-start.3 = (bf16[128,224]{0,1:T(8,128)(2,1)S(1)}, bf16[128,224]{0,1:T(8,128)(2,1)}, u32[]{:S(2)}) copy-start(bf16[128,224]{0,1:T(8,128)(2,1)} %param.19) | copy-start | bytes 172036
  105.1 29.9 %all-to-all-start.2 = ((f32[8,128,224]{1,2,0:T(8,128)}), f32[8,128,224]{1,2,0:T(8,128)S(1)}, u32[]{:S(2)}, u32[]{:S(2)}) async-start(f32[8,128,224]{1,2,0:T(8,128)} %broadcast_in_dim.59), calls=%async_computation.2 | async-start | bytes 1835008 | tf_op jit(solution)/shard_map/all_to_all | solution.py:37
  144.2 4.2 %copy-start.5 = (bf16[7168]{0:T(1024)(128)(2,1)S(1)}, bf16[7168]{0:T(1024)(128)(2,1)}, u32[]{:S(2)}) copy-start(bf16[7168]{0:T(1024)(128)(2,1)} %param.20) | copy-start | bytes 43012
  144.2 4.3 %copy-start.6 = (f32[128,8]{0,1:T(8,128)S(1)}, f32[128,8]{0,1:T(8,128)}, u32[]{:S(2)}) copy-start(f32[128,8]{0,1:T(8,128)} %param.25) | copy-start | bytes 12292
  144.2 21.2 %all-to-all-start.3 = ((bf16[32,64,224]{2,1,0:T(8,128)(2,1)}), bf16[32,64,224]{2,1,0:T(8,128)(2,1)S(1)}, u32[]{:S(2)}, u32[]{:S(2)}) async-start(bf16[32,64,224]{2,1,0:T(8,128)(2,1)} %bitcast.71), calls=%async_computation.3 | async-start | bytes 2097152 | tf_op jit(solution)/shard_map/all_to_all | solution.py:128
  176.7 47.5 %all-to-all-start.4 = ((f32[8,64,896]{2,1,0:T(8,128)}), f32[8,64,896]{2,1,0:T(8,128)}, u32[]{:S(2)}, u32[]{:S(2)}) async-start(f32[8,64,896]{2,1,0:T(8,128)} %multiply_bitcast_fusion), calls=%async_computation.4 | async-start | bytes 3670016 | tf_op jit(solution)/shard_map/all_to_all | solution.py:19
